TPU v7x, 32 devices: a whole 2x2x4 slice. The times are simulated.
32 devices in a mesh: section: 4 (over y, x), seq: 8 (over z, core).
Axes of the slice: x: 2, y: 2, z: 4, core: 2. Of those that a mesh axis runs over, the one named last changes fastest.
Arguments:
- stream: bfloat16 [4, 128, 1536], P('section', 'seq'), may hold values from -6 to 6
- queries: bfloat16 [4, 128, 1536], P('section', 'seq'), may hold values from -40 to 40
- fresh_keys: bfloat16 [4, 128, 1536], P('section', 'seq'), may hold values from -4 to 4
- fresh_values: bfloat16 [4, 128, 1536], P('section', 'seq'), may hold values from -6 to 6
- stale_keys: bfloat16 [4, 1536, 1536], P('section', 'seq'), may hold values from -6 to 6
- stale_values: bfloat16 [4, 1536, 1536], P('section', 'seq'), may hold values from -6 to 6
- gate: float32 [4, 1536], P('section'), may hold values from 0.5 to 4
- patch_of_section: int32 [4], P('section'), may hold values from 0 to 7, as said below
- text_len: int32 [1], replicated, may hold values from 128 to 512
Outputs:
- attended: bfloat16 [4, 128, 1536], P('section', 'seq')
- stream_next: bfloat16 [4, 128, 1536], P('section', 'seq')
Inputs may be any that keep to these rules, and one draw needn't show every extreme that they name: `patch_of_section`: section s works on patch (c - s) mod 8 for one c of the draw. The first text_len text positions are used.
All inputs are finite; a program needn't handle non-finite values.
Results may differ from a plain program's by a relative error of at most 0.0085.
Values may be sent and summed in bfloat16 or wider, within the bound.
A program may use at most 64 MiB of HBM per device.

v0:
```python
import math

import jax
import jax.numpy as jnp
from jax import lax
from jax.sharding import PartitionSpec as P

HEADS = 12
HDIM = 128
TXT = 512


FLOOR_SCORE = -1e30


def passed_along(value, axis, steps):
    count = lax.axis_size(axis)
    pairs = [(source, (source + steps) % count) for source in range(count)]
    return lax.ppermute(value, axis, pairs)


def head_scores(query_rows, key_rows):
    query_heads = query_rows.reshape(query_rows.shape[0], HEADS, HDIM)
    key_heads = key_rows.reshape(key_rows.shape[0], HEADS, HDIM)
    return jnp.einsum(
        "qhd,khd->hqk", query_heads, key_heads, preferred_element_type=jnp.float32
    ) / math.sqrt(HDIM)


def weighted_values(weights, value_rows):
    value_heads = value_rows.reshape(value_rows.shape[0], HEADS, HDIM)
    return jnp.einsum(
        "hqk,khd->qhd",
        weights.astype(jnp.bfloat16),
        value_heads,
        preferred_element_type=jnp.float32,
    )


def stale_allowed(first_row, piece_rows, patch_index, text_count, patch_length):
    positions = first_row + jnp.arange(piece_rows, dtype=jnp.int32)
    region = (positions - TXT) // patch_length
    return jnp.where(positions < TXT, positions < text_count, region != patch_index)


def local(
    stream,
    queries,
    fresh_keys,
    fresh_values,
    stale_keys,
    stale_values,
    gate,
    patch_of_section,
    text_len,
):
    incoming = passed_along(stream, "section", 1)
    row_count = queries.shape[1]
    patch_length = row_count * lax.axis_size("seq")
    patch_index = patch_of_section[0]
    text_count = text_len[0]
    everyone = lax.all_gather(queries, "seq", axis=1, tiled=True)[0]
    stale_rows = stale_keys.shape[1]
    key_rows = jnp.concatenate([stale_keys[0], fresh_keys[0]], 0)
    value_rows = jnp.concatenate([stale_values[0], fresh_values[0]], 0)
    first_row = lax.axis_index("seq") * stale_rows
    allowed = jnp.concatenate(
        [
            stale_allowed(first_row, stale_rows, patch_index, text_count, patch_length),
            jnp.ones((row_count,), dtype=bool),
        ],
        0,
    )
    scores = jnp.where(allowed[None, None, :], head_scores(everyone, key_rows), FLOOR_SCORE)
    local_max = jnp.max(scores, axis=2)
    global_max = lax.pmax(local_max, "seq")
    weights = jnp.where(allowed[None, None, :], jnp.exp(scores - local_max[:, :, None]), 0.0)
    factor = jnp.exp(local_max - global_max)
    partial_value = weighted_values(weights, value_rows) * jnp.transpose(factor)[:, :, None]
    partial_value = partial_value.reshape(patch_length, HEADS * HDIM)
    weight_sums = jnp.transpose(jnp.sum(weights, axis=2) * factor)
    weighted, row_sums = (
        lax.psum_scatter(partial_value, "seq", scatter_dimension=0, tiled=True),
        lax.psum_scatter(weight_sums, "seq", scatter_dimension=0, tiled=True),
    )
    averaged = weighted.reshape(row_count, HEADS, HDIM) / row_sums[:, :, None]
    attended = averaged.reshape(1, row_count, HEADS * HDIM).astype(jnp.bfloat16)
    stream_next = (
        incoming.astype(jnp.float32) + gate[:, None, :] * attended.astype(jnp.float32)
    ).astype(jnp.bfloat16)
    return (attended, stream_next)


def solution(mesh):
    placed = (
        P("section", "seq", None),
        P("section", "seq", None),
        P("section", "seq", None),
        P("section", "seq", None),
        P("section", "seq", None),
        P("section", "seq", None),
        P("section", None),
        P("section"),
        P(),
    )
    return jax.shard_map(
        local,
        mesh=mesh,
        in_specs=placed,
        out_specs=(P("section", "seq", None), P("section", "seq", None)),
        check_vma=False,
    )
```

profile of v0, /device:TPU:0, one launch (start us, length us, event | category | flops | bytes accessed | tf_op | source)
XLA Modules:
  0.0 116.1 jit_solution(6922269851643474781)
XLA Ops:
  7.2 0.0 reduce-scatter.7.cloned.1.call-start
  8.5 0.0 copy-start.1
  8.5 1.5 %concatenate.23 = bf16[192,12,128]{2,1,0:T(8,128)(2,1)S(1)} reshape(bf16[1,192,1536]{2,1,0:T(8,128)(2,1)} %param.13) | data formatting | bytes 1179648 | tf_op jit(solution)/shard_map/concatenate | solution.py:64
  10.0 0.0 copy-start.2
  10.0 0.2 copy.23
  10.2 0.0 copy-done.1
  10.2 16.2 %all_gather.3 = bf16[1,128,1536]{2,1,0:T(8,128)(2,1)S(1)} all-gather(bf16[1,16,1536]{2,1,0:T(8,128)(2,1)S(1)} %copy-done.1), channel_id=1, replica_groups=mesh['section'=4,'seq'=8] {'seq'}, dimensions={1}, use_global_device_ids=true | all-gather | bytes 442368 | tf_op jit(solution)/shard_map/all_gather | solution.py:62
  26.4 0.2 copy.25
  26.7 0.1 concatenate.24
  26.8 0.5 fusion.22
  27.3 0.0 copy-start
  27.3 17.3 %pmax.7 = f32[12,128]{1,0:T(8,128)S(1)} all-reduce(f32[12,128]{1,0:T(8,128)S(1)} %get-tuple-element.6), channel_id=1, replica_groups=mesh['section'=4,'seq'=8] {'seq'}, use_global_device_ids=true, to_apply=%region_1.2 | all-reduce | flops 1536 | bytes 12288 | tf_op jit(solution)/shard_map/pmax | solution.py:76
  44.6 0.2 fusion.3
  44.9 0.7 copy.30
  45.6 0.0 reduce-scatter.7.cloned.1.call-update
  45.7 0.0 copy-start.3
  45.7 0.0 reduce-scatter.5.cloned.1.call-start
  45.7 0.4 concatenate.19
  46.2 0.2 copy.21
  46.3 0.2 copy-done.3
  46.5 0.1 concatenate.20
  46.6 0.5 fusion.2
  47.0 0.0 copy-start.5
  47.1 0.0 copy-start.4
  47.1 1.1 copy.27
  48.2 0.0 reduce-scatter.5.cloned.1.call-update
  48.3 1.5 %collective-permute-start = (bf16[1,16,1536]{2,1,0:T(8,128)(2,1)S(1)}, bf16[1,16,1536]{2,1,0:T(8,128)(2,1)S(1)}, u32[]{:S(2)}, u32[]{:S(2)}) collective-permute-start(bf16[1,16,1536]{2,1,0:T(8,128)(2,1)S(1)} %copy-done.5), channel_id=1, source_target_pairs={{0,8},{8,16},{16,24},{24,0},{1,9},{9,17},{17,25},{25,1},{2,10},{10... | collective-permute-start | bytes 147464 | tf_op jit(solution)/shard_map/ppermute | solution.py:19
  49.8 24.8 %reduce-scatter.7.cloned.1.call-done = f32[16,12]{1,0:T(8,128)} async-done(((f32[128,12]{1,0:T(8,128)}), f32[16,12]{1,0:T(8,128)}) %reduce-scatter.7.cloned.1.call-update) | async-done | bytes 784 | tf_op jit(solution)/shard_map/reduce_scatter | solution.py:84
  74.6 0.0 collective-permute-done
  74.6 32.3 %reduce-scatter.5.cloned.1.call-done = f32[16,1536]{1,0:T(8,128)} async-done(((f32[128,1536]{1,0:T(8,128)}), f32[16,1536]{1,0:T(8,128)}) %reduce-scatter.5.cloned.1.call-update) | async-done | bytes 98320 | tf_op jit(solution)/shard_map/reduce_scatter | solution.py:83
  106.9 0.8 div.35
  107.7 1.6 %fusion.16 = (bf16[1,16,1536]{2,1,0:T(8,128)(2,1)}, bf16[16,1536]{1,0:T(8,128)(2,1)}) fusion(bf16[1,16,1536]{2,1,0:T(8,128)(2,1)S(1)} %collective-permute-done, f32[1536]{0:T(1024)S(1)} %reduce, f32[16,1536]{1,0:T(8,128)} %reduce-scatter.5.cloned.1.call-done, f32[2,8,12,128]{3,2,1,0:T(8,128)S(1)} %bitcast.30), kind=kLoop, calls=%fused_computation.20 | loop fusion | flops 172032 | bytes 350208 | tf_op jit(solution)/shard_map/convert_element_type | solution.py:90
  (10 shorter events, 0.1 us)
Async XLA Ops:
  7.2 67.4 %reduce-scatter.7.cloned.1.call-start = ((), (), s32[]{:S(2)}) async-start(), calls=%async_computation.3 | async-start | bytes 73728 | tf_op jit(solution)/shard_map/reduce_scatter | solution.py:84
  8.5 1.7 %copy-start.1 = (bf16[1,16,1536]{2,1,0:T(8,128)(2,1)S(1)}, bf16[1,16,1536]{2,1,0:T(8,128)(2,1)}, u32[]{:S(2)}) copy-start(bf16[1,16,1536]{2,1,0:T(8,128)(2,1)} %param.10) | copy-start | bytes 147460
  10.0 16.6 %copy-start.2 = (bf16[1,16,1536]{2,1,0:T(8,128)(2,1)S(1)}, bf16[1,16,1536]{2,1,0:T(8,128)(2,1)}, u32[]{:S(2)}) copy-start(bf16[1,16,1536]{2,1,0:T(8,128)(2,1)} %param.11) | copy-start | bytes 147460
  27.3 18.4 %copy-start = (bf16[1,192,1536]{2,1,0:T(8,128)(2,1)S(1)}, bf16[1,192,1536]{2,1,0:T(8,128)(2,1)}, u32[]{:S(2)}) copy-start(bf16[1,192,1536]{2,1,0:T(8,128)(2,1)} %param.14) | copy-start | bytes 1769476
  45.7 0.8 copy-start.3
  45.7 61.2 %reduce-scatter.5.cloned.1.call-start = ((), (), s32[]{:S(2)}) async-start(), calls=%async_computation.2 | async-start | bytes 884736 | tf_op jit(solution)/shard_map/reduce_scatter | solution.py:83
  47.0 1.2 %copy-start.5 = (bf16[1,16,1536]{2,1,0:T(8,128)(2,1)S(1)}, bf16[1,16,1536]{2,1,0:T(8,128)(2,1)}, u32[]{:S(2)}) copy-start(bf16[1,16,1536]{2,1,0:T(8,128)(2,1)} %param.9) | copy-start | bytes 147460
  47.1 2.7 %copy-start.4 = (f32[1,1536]{1,0:T(1,128)S(1)}, f32[1,1536]{1,0:T(1,128)}, u32[]{:S(2)}) copy-start(f32[1,1536]{1,0:T(1,128)} %param.15) | copy-start | bytes 18436
  48.3 26.3 %collective-permute-start = (bf16[1,16,1536]{2,1,0:T(8,128)(2,1)S(1)}, bf16[1,16,1536]{2,1,0:T(8,128)(2,1)S(1)}, u32[]{:S(2)}, u32[]{:S(2)}) collective-permute-start(bf16[1,16,1536]{2,1,0:T(8,128)(2,1)S(1)} %copy-done.5), channel_id=1, source_target_pairs={{0,8},{8,16},{16,24},{24,0},{1,9},{9,17},{17,25},{25,1},{2,10},{10... | collective-permute-start | bytes 147464 | tf_op jit(solution)/shard_map/ppermute | solution.py:19
Sparse Core Ops, SparseCore 0:
  45.8 28.7 reduce-scatter.6
  76.9 30.0 reduce-scatter.4
where the time goes:
time: 116 us
  waiting for transfers between devices  57.1 us (49%)
  blocking collectives  33.6 us (29%)
  between operations  15.5 us (13%)
  local copies, waits for them, and re-layouts  5.43 us (5%)
  other arithmetic  1.87 us (2%)
  starting transfers between devices  1.63 us (1%)
    reduce_scatter x1, waiting for transfers between devices, local(): lax.psum_scatter(partial_value, 'seq', scatter_dimension=0, tiled=True)  32.3 us
    reduce_scatter x1, waiting for transfers between devices, local(): lax.psum_scatter(weight_sums, 'seq', scatter_dimension=0, tiled=True)  24.8 us
    pmax x1, blocking collectives, local(): global_max = lax.pmax(local_max, 'seq')  17.3 us
    all_gather x1, blocking collectives, local(): everyone = lax.all_gather(queries, 'seq', axis=1, tiled=True)[0]  16.2 us
  transfers between devices with their start and end apart: 3, of which 2 were waited for; matrix products, arithmetic and copies ran while one was open for 2% of the time, Pallas kernels for 0%

commit v1 on v0

v1 whole, which is shorter than its diff:
```python
import functools
import math

import jax
import jax.numpy as jnp
from jax import lax
from jax.experimental import pallas as pl
from jax.experimental.pallas import tpu as pltpu
from jax.sharding import PartitionSpec as P

HEADS = 12
HDIM = 128
TXT = 512
CORES = 2
HALF = HEADS // CORES
TILES = HALF + 1
LANES = 128
STATS = 8
FLOOR_SCORE = -1e30
SCALE = math.log2(math.e) / math.sqrt(HDIM)
MESH = pl.DeviceIdType.MESH


def query_groups(chips):
    return [list(range(chips))]


def kernel(
    sections,
    chips,
    stream,
    queries,
    fresh_keys,
    fresh_values,
    stale_keys,
    stale_values,
    gate,
    patch_of_section,
    text_len,
    attended_ref,
    stream_ref,
    own_queries,
    all_queries,
    key_rows,
    value_rows,
    part,
    got,
    incoming,
    gate_row,
    patch_scalar,
    text_scalar,
    local_sem,
    query_send,
    query_recv,
    cache_send,
    cache_recv,
    part_send,
    part_recv,
    stream_sem,
):
    me = lax.axis_index("seq")
    section = lax.axis_index("section")
    core = lax.rem(me, CORES)
    chip = me // CORES
    other = 1 - core
    partner = chip * CORES + other
    rows = queries.shape[1]
    stale = stale_keys.shape[1]
    width = HALF * HDIM
    patch_length = rows * chips * CORES

    def columns(which):
        return pl.ds(pl.multiple_of(which * width, width), width)

    def row_slice(start, size):
        return pl.ds(pl.multiple_of(start, 16), size)

    def device(offset, which):
        return lax.rem(chip + offset, chips) * CORES + which

    locals_ = [
        pltpu.make_async_copy(queries.at[0], own_queries, local_sem.at[0]),
        pltpu.make_async_copy(
            queries.at[0, :, columns(core)],
            all_queries.at[row_slice(core * rows, rows)],
            local_sem.at[1],
        ),
        pltpu.make_async_copy(gate, gate_row, local_sem.at[2]),
        pltpu.make_async_copy(patch_of_section, patch_scalar, local_sem.at[3]),
        pltpu.make_async_copy(text_len, text_scalar, local_sem.at[4]),
        pltpu.make_async_copy(
            stale_keys.at[0, :, columns(core)], key_rows.at[pl.ds(0, stale)], local_sem.at[5]
        ),
        pltpu.make_async_copy(
            fresh_keys.at[0, :, columns(core)], key_rows.at[pl.ds(stale, rows)], local_sem.at[6]
        ),
        pltpu.make_async_copy(
            stale_values.at[0, :, columns(core)], value_rows.at[pl.ds(0, stale)], local_sem.at[7]
        ),
        pltpu.make_async_copy(
            fresh_values.at[0, :, columns(core)], value_rows.at[pl.ds(stale, rows)], local_sem.at[8]
        ),
    ]
    for copy in locals_:
        copy.start()

    barrier = pltpu.get_barrier_semaphore()
    for offset in range(chips):
        for which in range(CORES):
            if offset == 0:
                continue
            pl.semaphore_signal(
                barrier, inc=1, device_id={"seq": device(offset, which)}, device_id_type=MESH
            )
    pl.semaphore_signal(barrier, inc=1, device_id={"seq": partner}, device_id_type=MESH)
    pl.semaphore_signal(
        barrier,
        inc=1,
        device_id={"section": lax.rem(section + sections - 1, sections)},
        device_id_type=MESH,
    )
    locals_[0].wait()
    pl.semaphore_wait(barrier, chips * CORES)

    query_copies = []
    for offset in list(range(1, chips)) + [0]:
        back = (chips - offset) % chips
        for which in range(CORES) if offset else (other,):
            target = device(offset, which)
            query_copies.append(
                pltpu.make_async_remote_copy(
                    src_ref=own_queries.at[:, columns(which)],
                    dst_ref=all_queries.at[row_slice(back * CORES * rows + core * rows, rows)],
                    send_sem=query_send.at[offset, which],
                    recv_sem=query_recv.at[back, core],
                    device_id={"seq": target},
                    device_id_type=MESH,
                )
            )
            query_copies[-1].start()

    base = stale + rows
    cache_copies = []
    for number, (source, start, size, target) in enumerate(
        (
            (stale_keys, base, stale, key_rows),
            (fresh_keys, base + stale, rows, key_rows),
            (stale_values, base, stale, value_rows),
            (fresh_values, base + stale, rows, value_rows),
        )
    ):
        cache_copies.append(
            pltpu.make_async_remote_copy(
                src_ref=source.at[0, :, columns(other)],
                dst_ref=target.at[pl.ds(start, size)],
                send_sem=cache_send.at[number],
                recv_sem=cache_recv.at[number],
                device_id={"seq": partner},
                device_id_type=MESH,
            )
        )
        cache_copies[-1].start()

    stream_copy = pltpu.make_async_remote_copy(
        src_ref=stream.at[0],
        dst_ref=incoming,
        send_sem=stream_sem.at[0],
        recv_sem=stream_sem.at[1],
        device_id={"section": lax.rem(section + 1, sections)},
        device_id_type=MESH,
    )
    stream_copy.start()

    for copy in locals_[1:]:
        copy.wait()

    total = CORES * base
    column = lax.broadcasted_iota(jnp.int32, (1, total), 1)
    second = column >= base
    inner = jnp.where(second, column - base, column)
    owner = jnp.where(second, partner, me)
    position = owner * stale + inner
    first_banned = TXT + patch_scalar[0] * patch_length
    banned = (position >= first_banned) & (position < first_banned + patch_length)
    unused_text = (position < TXT) & (position >= text_scalar[0])
    banned = (banned & (position >= TXT)) | unused_text
    allowed = (inner >= stale) | jnp.logical_not(banned)
    penalty = jnp.where(allowed, 0.0, FLOOR_SCORE)

    for number in range(4):
        cache_copies[number].wait_recv()

    part_copies = []
    own_copy = None
    for group in query_groups(chips):
        for offset in group:
            for which in range(CORES) if offset else (other,):
                pltpu.make_async_remote_copy(
                    src_ref=own_queries.at[:, columns(which)],
                    dst_ref=all_queries.at[row_slice(offset * CORES * rows + which * rows, rows)],
                    send_sem=query_send.at[offset, which],
                    recv_sem=query_recv.at[offset, which],
                    device_id={"seq": device(offset, which)},
                    device_id_type=MESH,
                ).wait_recv()
        low = group[0] * CORES * rows
        count = len(group) * CORES * rows
        span = pl.ds(low, count)
        lane = lax.broadcasted_iota(jnp.int32, (count, LANES), 1)
        lane_head = lax.rem(lane, STATS)
        spread = jnp.zeros((count, LANES), jnp.float32)
        for head in range(HALF):
            wide = pl.ds(head * HDIM, HDIM)
            scores = lax.dot_general(
                all_queries[span, wide],
                key_rows[:, wide],
                (((1,), (1,)), ((), ())),
                preferred_element_type=jnp.float32,
            )
            scores = scores * SCALE + penalty
            largest = jnp.max(scores, axis=1, keepdims=True)
            weights = jnp.exp2(scores - largest)
            amount = jnp.sum(weights, axis=1, keepdims=True)
            summed = jnp.dot(
                weights.astype(jnp.bfloat16),
                value_rows[:, wide],
                preferred_element_type=jnp.float32,
            )
            part[head, span] = (summed / amount).astype(jnp.bfloat16)
            spread = jnp.where(lane_head == head, largest + jnp.log2(amount), spread)
        high = spread.astype(jnp.bfloat16).astype(jnp.float32)
        rest = spread - high
        middle = rest.astype(jnp.bfloat16).astype(jnp.float32)
        low_term = rest - middle
        part[HALF, span] = jnp.where(
            lane < STATS, high, jnp.where(lane < 2 * STATS, middle, low_term)
        ).astype(jnp.bfloat16)
        for offset in group:
            back = (chips - offset) % chips
            for which in range(CORES) if offset else (other,):
                copy = pltpu.make_async_remote_copy(
                    src_ref=part.at[:, row_slice(offset * CORES * rows + which * rows, rows)],
                    dst_ref=got.at[back, core],
                    send_sem=part_send.at[offset, which],
                    recv_sem=part_recv.at[back, core],
                    device_id={"seq": device(offset, which)},
                    device_id_type=MESH,
                )
                copy.start()
                part_copies.append(copy)
            if offset == 0:
                own_copy = pltpu.make_async_copy(
                    part.at[:, row_slice(core * rows, rows)], got.at[0, core], local_sem.at[9]
                )
                own_copy.start()

    own_copy.wait()
    stream_copy.wait_recv()
    for offset in range(chips):
        for which in range(CORES) if offset else (other,):
            pltpu.make_async_remote_copy(
                src_ref=part.at[:, row_slice(which * rows, rows)],
                dst_ref=got.at[offset, which],
                send_sem=part_send.at[offset, which],
                recv_sem=part_recv.at[offset, which],
                device_id={"seq": device(offset, which)},
                device_id_type=MESH,
            ).wait_recv()

    for which in range(CORES):
        logs = []
        for offset in range(chips):
            terms = got[offset, which, HALF].astype(jnp.float32)
            logs.append(
                terms
                + pltpu.roll(terms, LANES - STATS, 1)
                + pltpu.roll(terms, LANES - 2 * STATS, 1)
            )
        largest = functools.reduce(jnp.maximum, logs)
        shares = [jnp.exp2(log - largest) for log in logs]
        whole = functools.reduce(jnp.add, shares)
        shares = [share / whole for share in shares]
        for head in range(HALF):
            wide = pl.ds((which * HALF + head) * HDIM, HDIM)
            mean = functools.reduce(
                jnp.add,
                [
                    shares[offset][:, head : head + 1]
                    * got[offset, which, head].astype(jnp.float32)
                    for offset in range(chips)
                ],
            )
            rounded = mean.astype(jnp.bfloat16)
            attended_ref[0, :, wide] = rounded
            stream_ref[0, :, wide] = (
                incoming[:, wide].astype(jnp.float32)
                + gate_row[:, wide] * rounded.astype(jnp.float32)
            ).astype(jnp.bfloat16)

    for copy in query_copies + cache_copies + [stream_copy] + part_copies:
        copy.wait_send()


def local(*arguments):
    sections = lax.axis_size("section")
    count = lax.axis_size("seq")
    chips = count // CORES
    queries, stale_keys = arguments[1], arguments[4]
    rows, channels = queries.shape[1:]
    cached = CORES * (stale_keys.shape[1] + rows)
    width = HALF * HDIM
    everyone = rows * count
    anywhere = pl.BlockSpec(memory_space=pl.ANY)
    inside = pl.BlockSpec(memory_space=pltpu.VMEM)
    result = jax.ShapeDtypeStruct((1, rows, channels), jnp.bfloat16)
    return pl.pallas_call(
        functools.partial(kernel, sections, chips),
        out_shape=(result, result),
        in_specs=[anywhere] * 9,
        out_specs=(inside, inside),
        scratch_shapes=[
            pltpu.VMEM((rows, channels), jnp.bfloat16),
            pltpu.VMEM((everyone, width), jnp.bfloat16),
            pltpu.VMEM((cached, width), jnp.bfloat16),
            pltpu.VMEM((cached, width), jnp.bfloat16),
            pltpu.VMEM((TILES, everyone, HDIM), jnp.bfloat16),
            pltpu.VMEM((chips, CORES, TILES, rows, HDIM), jnp.bfloat16),
            pltpu.VMEM((rows, channels), jnp.bfloat16),
            pltpu.VMEM((1, channels), jnp.float32),
            pltpu.SMEM((1,), jnp.int32),
            pltpu.SMEM((1,), jnp.int32),
            pltpu.SemaphoreType.DMA((10,)),
            pltpu.SemaphoreType.DMA((chips, CORES)),
            pltpu.SemaphoreType.DMA((chips, CORES)),
            pltpu.SemaphoreType.DMA((4,)),
            pltpu.SemaphoreType.DMA((4,)),
            pltpu.SemaphoreType.DMA((chips, CORES)),
            pltpu.SemaphoreType.DMA((chips, CORES)),
            pltpu.SemaphoreType.DMA((2,)),
        ],
        compiler_params=pltpu.CompilerParams(collective_id=0, has_side_effects=True),
    )(*arguments)


def solution(mesh):
    placed = (
        P("section", "seq", None),
        P("section", "seq", None),
        P("section", "seq", None),
        P("section", "seq", None),
        P("section", "seq", None),
        P("section", "seq", None),
        P("section", None),
        P("section"),
        P(),
    )
    return jax.shard_map(
        local,
        mesh=mesh,
        in_specs=placed,
        out_specs=(P("section", "seq", None), P("section", "seq", None)),
        check_vma=False,
    )
```

time: 116 us -> 22.8 us (0.20)
  waiting for transfers between devices: 57.1 us -> 0 us
  blocking collectives: 33.6 us -> 0 us
  Pallas kernels: 0 us -> 18.6 us
  between operations: 15.5 us -> 1.94 us
  local copies, waits for them, and re-layouts: 5.43 us -> 2.06 us
  other arithmetic: 1.87 us -> 0 us
  starting transfers between devices: 1.63 us -> 0 us
    reduce_scatter x2 -> x0, waiting for transfers between devices: 57.1 us -> none  [the longest x1 32.3 us: local(): lax.psum_scatter(partial_value, 'seq', scatter_dimension=0, tiled=True)]
    pallas_call x0 -> x1, Pallas kernels: none -> 18.6 us  [local(): pl.pallas_call(functools.partial(kernel, sections, chips), out_shape=(res...]
    pmax x1 -> x0, blocking collectives: 17.3 us -> none  [local(): global_max = lax.pmax(local_max, 'seq')]
    all_gather x1 -> x0, blocking collectives: 16.2 us -> none  [local(): everyone = lax.all_gather(queries, 'seq', axis=1, tiled=True)[0]]
    concatenate x9 -> x0, local copies, waits for them, and re-layouts: 2.37 us -> none  [the longest x4 1.73 us: local(): key_rows = jnp.concatenate([stale_keys[0], fresh_keys[0]], 0)]
    convert_element_type x1 -> x0, other arithmetic: 1.58 us -> none  [local(): stream_next = (incoming.astype(jnp.float32) + gate[:, None, :] * attended...]
    ppermute x1 -> x0, starting transfers between devices: 1.55 us -> none  [passed_along(): return lax.ppermute(value, axis, pairs)]
  transfers between devices with their start and end apart: 3 -> 0, of which waited for: 2 -> 0; matrix products, arithmetic and copies ran while one was open for 2% -> 0% of each run, Pallas kernels for 0% -> 0%
where the time goes in v1:
time: 22.8 us; the launch traced here: 22.6 us
  Pallas kernels  18.6 us (82%)
  local copies, waits for them, and re-layouts  2.06 us (9%)
  between operations  1.94 us (9%)
    pallas_call x1, Pallas kernels, local(): pl.pallas_call(functools.partial(kernel, sections, chips), out_shape=(res...  18.6 us
    unnamed x4, local copies, waits for them, and re-layouts  2.06 us

profile of v1, /device:TPU:0, one launch (start us, length us, event | category | flops | bytes accessed | tf_op | source)
XLA Modules:
  0.0 22.6 jit_solution(3801210792135362415)
XLA Ops:
  1.9 18.6 %shard_map.104 = (bf16[1,16,1536]{2,1,0:T(8,128)(2,1)}, bf16[1,16,1536]{2,1,0:T(8,128)(2,1)}) custom-call(bf16[1,16,1536]{2,1,0:T(8,128)(2,1)} %stream.1, bf16[1,16,1536]{2,1,0:T(8,128)(2,1)} %queries.1, bf16[1,16,1536]{2,1,0:T(8,128)(2,1)} %fresh_keys.1, bf16[1,16,1536]{2,1,0:T(8,128)(2,1)} %fresh_values.1, bf16[1,192,1536]{2,1,0:T(8,128)(2,1)} %stale_keys.1, ...), custom_call_target="tpu_custom_call" | custom-call | tf_op jit(solution)/shard_map/pallas_call | solution.py:316
  20.5 0.0 copy-start
  20.5 1.4 %copy.15 = bf16[1,16,1536]{2,1,0:T(8,128)(2,1)} copy(bf16[1,16,1536]{2,1,0:T(8,128)(2,1)} %get-tuple-element.4) | data formatting | bytes 98304
  22.0 0.0 copy-done
  22.0 0.6 %copy.16 = bf16[1,16,1536]{2,1,0:T(8,128)(2,1)} copy(bf16[1,16,1536]{2,1,0:T(8,128)(2,1)S(1)} %copy-done) | data formatting | bytes 98304
Async XLA Ops:
  20.5 1.4 %copy-start = (bf16[1,16,1536]{2,1,0:T(8,128)(2,1)S(1)}, bf16[1,16,1536]{2,1,0:T(8,128)(2,1)}, u32[]{:S(2)}) copy-start(bf16[1,16,1536]{2,1,0:T(8,128)(2,1)} %get-tuple-element.5) | copy-start | bytes 147460

commit v2 on v1

--- a/solution.py
+++ b/solution.py
@@ -22,7 +22,7 @@
 
 
 def query_groups(chips):
-    return [list(range(chips))]
+    return [[0], list(range(1, chips))]
 
 
 def kernel(
@@ -37,8 +37,7 @@
     gate,
     patch_of_section,
     text_len,
-    attended_ref,
-    stream_ref,
+    results,
     own_queries,
     all_queries,
     key_rows,
@@ -291,8 +290,8 @@
                 ],
             )
             rounded = mean.astype(jnp.bfloat16)
-            attended_ref[0, :, wide] = rounded
-            stream_ref[0, :, wide] = (
+            results[0, 0, :, wide] = rounded
+            results[1, 0, :, wide] = (
                 incoming[:, wide].astype(jnp.float32)
                 + gate_row[:, wide] * rounded.astype(jnp.float32)
             ).astype(jnp.bfloat16)
@@ -312,12 +311,12 @@
     everyone = rows * count
     anywhere = pl.BlockSpec(memory_space=pl.ANY)
     inside = pl.BlockSpec(memory_space=pltpu.VMEM)
-    result = jax.ShapeDtypeStruct((1, rows, channels), jnp.bfloat16)
-    return pl.pallas_call(
+    result = pltpu.VMEM((2, 1, rows, channels), jnp.bfloat16)
+    results = pl.pallas_call(
         functools.partial(kernel, sections, chips),
-        out_shape=(result, result),
+        out_shape=result,
         in_specs=[anywhere] * 9,
-        out_specs=(inside, inside),
+        out_specs=inside,
         scratch_shapes=[
             pltpu.VMEM((rows, channels), jnp.bfloat16),
             pltpu.VMEM((everyone, width), jnp.bfloat16),
@@ -340,6 +339,7 @@
         ],
         compiler_params=pltpu.CompilerParams(collective_id=0, has_side_effects=True),
     )(*arguments)
+    return (results[0], results[1])
 
 
 def solution(mesh):

time: 22.8 us -> 20.7 us (0.908)
  local copies, waits for them, and re-layouts: 2.06 us -> 0.64 us
  Pallas kernels: 18.6 us -> 17.9 us
    unnamed x4 -> x0, local copies, waits for them, and re-layouts: 2.06 us -> none
    pallas_call x1, Pallas kernels: 18.6 us -> 17.9 us  [local(): pl.pallas_call(functools.partial(kernel, sections, chips), out_shape=resu...]
    squeeze x0 -> x1, local copies, waits for them, and re-layouts: none -> 0.64 us  [local(): return (results[0], results[1])]
where the time goes in v2:
time: 20.7 us; the launch traced here: 20.5 us
  Pallas kernels  17.9 us (86%)
  between operations  1.93 us (9%)
  local copies, waits for them, and re-layouts  0.64 us (3%)
    pallas_call x1, Pallas kernels, local(): pl.pallas_call(functools.partial(kernel, sections, chips), out_shape=resu...  17.9 us
    squeeze x1, local copies, waits for them, and re-layouts, local(): return (results[0], results[1])  0.64 us

profile of v2, /device:TPU:0, one launch (start us, length us, event | category | flops | bytes accessed | tf_op | source)
XLA Modules:
  0.0 20.5 jit_solution(5607117487134130066)
XLA Ops:
  1.9 17.9 %shard_map.104 = bf16[2,1,16,1536]{3,2,1,0:T(8,128)(2,1)S(1)} custom-call(bf16[1,16,1536]{2,1,0:T(8,128)(2,1)} %stream.1, bf16[1,16,1536]{2,1,0:T(8,128)(2,1)} %queries.1, bf16[1,16,1536]{2,1,0:T(8,128)(2,1)} %fresh_keys.1, bf16[1,16,1536]{2,1,0:T(8,128)(2,1)} %fresh_values.1, bf16[1,192,1536]{2,1,0:T(8,128)(2,1)} %stale_keys.1, ...), custom_call_target="tpu_custom_call" | custom-call | tf_op jit(solution)/shard_map/pallas_call | solution.py:315
  19.9 0.6 %slice_bitcast_fusion = (bf16[1,16,1536]{2,1,0:T(8,128)(2,1)}, bf16[1,16,1536]{2,1,0:T(8,128)(2,1)}) fusion(bf16[2,1,16,1536]{3,2,1,0:T(8,128)(2,1)S(1)} %shard_map.104), kind=kLoop, calls=%fused_computation | loop fusion | bytes 196608 | tf_op jit(solution)/shard_map/squeeze | solution.py:342

commit v3 on v2

--- a/solution.py
+++ b/solution.py
@@ -77,32 +77,6 @@
     def device(offset, which):
         return lax.rem(chip + offset, chips) * CORES + which
 
-    locals_ = [
-        pltpu.make_async_copy(queries.at[0], own_queries, local_sem.at[0]),
-        pltpu.make_async_copy(
-            queries.at[0, :, columns(core)],
-            all_queries.at[row_slice(core * rows, rows)],
-            local_sem.at[1],
-        ),
-        pltpu.make_async_copy(gate, gate_row, local_sem.at[2]),
-        pltpu.make_async_copy(patch_of_section, patch_scalar, local_sem.at[3]),
-        pltpu.make_async_copy(text_len, text_scalar, local_sem.at[4]),
-        pltpu.make_async_copy(
-            stale_keys.at[0, :, columns(core)], key_rows.at[pl.ds(0, stale)], local_sem.at[5]
-        ),
-        pltpu.make_async_copy(
-            fresh_keys.at[0, :, columns(core)], key_rows.at[pl.ds(stale, rows)], local_sem.at[6]
-        ),
-        pltpu.make_async_copy(
-            stale_values.at[0, :, columns(core)], value_rows.at[pl.ds(0, stale)], local_sem.at[7]
-        ),
-        pltpu.make_async_copy(
-            fresh_values.at[0, :, columns(core)], value_rows.at[pl.ds(stale, rows)], local_sem.at[8]
-        ),
-    ]
-    for copy in locals_:
-        copy.start()
-
     barrier = pltpu.get_barrier_semaphore()
     for offset in range(chips):
         for which in range(CORES):
@@ -118,6 +92,32 @@
         device_id={"section": lax.rem(section + sections - 1, sections)},
         device_id_type=MESH,
     )
+    locals_ = [
+        pltpu.make_async_copy(queries.at[0], own_queries, local_sem.at[0]),
+        pltpu.make_async_copy(
+            queries.at[0, :, columns(core)],
+            all_queries.at[row_slice(core * rows, rows)],
+            local_sem.at[1],
+        ),
+        pltpu.make_async_copy(gate, gate_row, local_sem.at[2]),
+        pltpu.make_async_copy(patch_of_section, patch_scalar, local_sem.at[3]),
+        pltpu.make_async_copy(text_len, text_scalar, local_sem.at[4]),
+        pltpu.make_async_copy(
+            stale_keys.at[0, :, columns(core)], key_rows.at[pl.ds(0, stale)], local_sem.at[5]
+        ),
+        pltpu.make_async_copy(
+            fresh_keys.at[0, :, columns(core)], key_rows.at[pl.ds(stale, rows)], local_sem.at[6]
+        ),
+        pltpu.make_async_copy(
+            stale_values.at[0, :, columns(core)], value_rows.at[pl.ds(0, stale)], local_sem.at[7]
+        ),
+        pltpu.make_async_copy(
+            fresh_values.at[0, :, columns(core)], value_rows.at[pl.ds(stale, rows)], local_sem.at[8]
+        ),
+    ]
+    for copy in locals_:
+        copy.start()
+
     locals_[0].wait()
     pl.semaphore_wait(barrier, chips * CORES)
 

time: 20.7 us -> 20.7 us (level)
  no operation moved by 1% of the time
where the time goes in v3:
time: 20.7 us; the launch traced here: 20.5 us
  Pallas kernels  17.9 us (86%)
  between operations  1.93 us (9%)
  local copies, waits for them, and re-layouts  0.64 us (3%)
    pallas_call x1, Pallas kernels, local(): pl.pallas_call(functools.partial(kernel, sections, chips), out_shape=resu...  17.9 us
    squeeze x1, local copies, waits for them, and re-layouts, local(): return (results[0], results[1])  0.64 us

profile of v3, /device:TPU:0, one launch (start us, length us, event | category | flops | bytes accessed | tf_op | source)
XLA Modules:
  0.0 20.5 jit_solution(11747999675922077551)
XLA Ops:
  1.9 17.9 %shard_map.104 = bf16[2,1,16,1536]{3,2,1,0:T(8,128)(2,1)S(1)} custom-call(bf16[1,16,1536]{2,1,0:T(8,128)(2,1)} %stream.1, bf16[1,16,1536]{2,1,0:T(8,128)(2,1)} %queries.1, bf16[1,16,1536]{2,1,0:T(8,128)(2,1)} %fresh_keys.1, bf16[1,16,1536]{2,1,0:T(8,128)(2,1)} %fresh_values.1, bf16[1,192,1536]{2,1,0:T(8,128)(2,1)} %stale_keys.1, ...), custom_call_target="tpu_custom_call" | custom-call | tf_op jit(solution)/shard_map/pallas_call | solution.py:315
  19.9 0.6 %slice_bitcast_fusion = (bf16[1,16,1536]{2,1,0:T(8,128)(2,1)}, bf16[1,16,1536]{2,1,0:T(8,128)(2,1)}) fusion(bf16[2,1,16,1536]{3,2,1,0:T(8,128)(2,1)S(1)} %shard_map.104), kind=kLoop, calls=%fused_computation | loop fusion | bytes 196608 | tf_op jit(solution)/shard_map/squeeze | solution.py:342
